TPU v7x, 8 devices: a whole 2x2x1 slice. The times are simulated.
8 devices in a mesh: data: 8 (over z, y, x, core).
Axes of the slice: x: 2, y: 2, z: 1, core: 2. Of those that a mesh axis runs over, the one named last changes fastest.
Arguments:
- x_init: bfloat16 [256, 128, 768], P('data')
- cot_out: bfloat16 [256, 128, 768], P('data')
- w_query: bfloat16 [6, 768, 768], replicated
- w_key: bfloat16 [6, 768, 768], replicated
- w_value: bfloat16 [6, 768, 768], replicated
- w_proj: bfloat16 [6, 768, 768], replicated
- w_up: bfloat16 [768, 3072], replicated
- w_down: bfloat16 [3072, 768], replicated
Outputs:
- output 1: float32 [6, 768, 768], replicated
- output 2: float32 [6, 768, 768], replicated
- output 3: float32 [6, 768, 768], replicated
- output 4: float32 [6, 768, 768], replicated
- output 5: float32 [768, 3072], replicated
- output 6: float32 [3072, 768], replicated
- output 7: bfloat16 [256, 128, 768], P('data')
All inputs are finite; a program needn't handle non-finite values.
Results may differ from a plain program's by a relative error of at most 0.02.
Values are sent between devices in bfloat16 or wider.
A program may use at most 1 GiB of HBM per device.

v0:
```python
import jax
import jax.numpy as jnp
from jax import lax
from jax.sharding import PartitionSpec as P

EPS = 1e-6
HEAD_DIM = 64


def rms_norm(x_f32):
    return x_f32 * lax.rsqrt(jnp.mean(x_f32 * x_f32, axis=-1, keepdims=True) + EPS)


def gelu_tanh(pre_f32):
    return jax.nn.gelu(pre_f32, approximate=True)


def product(subscripts, lhs, rhs):
    return jnp.einsum(subscripts, lhs, rhs, preferred_element_type=jnp.float32)


def layer_forward(x_act, w_query, w_key, w_value, w_proj, w_up, w_down, heads):
    batch, seq_len, width = x_act.shape
    head_dim = width // heads
    x_f32 = x_act.astype(jnp.float32)
    normed = rms_norm(x_f32).astype(jnp.bfloat16)
    query = product("bsd,de->bse", normed, w_query).astype(jnp.bfloat16).reshape(batch, seq_len, heads, head_dim)
    key_act = product("bsd,de->bse", normed, w_key).astype(jnp.bfloat16).reshape(batch, seq_len, heads, head_dim)
    value = product("bsd,de->bse", normed, w_value).astype(jnp.bfloat16).reshape(batch, seq_len, heads, head_dim)
    scores = product("bqhd,bkhd->bhqk", query, key_act) * head_dim ** -0.5
    probs = jax.nn.softmax(scores, axis=-1).astype(jnp.bfloat16)
    mixed = product("bhqk,bkhd->bqhd", probs, value).astype(jnp.bfloat16).reshape(batch, seq_len, width)
    attn_out = product("bsd,de->bse", mixed, w_proj).astype(jnp.bfloat16)
    hidden = (x_f32 + attn_out.astype(jnp.float32)).astype(jnp.bfloat16)
    normed2 = rms_norm(hidden.astype(jnp.float32)).astype(jnp.bfloat16)
    pre_act = product("bsd,df->bsf", normed2, w_up).astype(jnp.bfloat16)
    activated = gelu_tanh(pre_act.astype(jnp.float32)).astype(jnp.bfloat16)
    mlp_out = product("bsf,fd->bsd", activated, w_down).astype(jnp.bfloat16)
    x_next = (hidden.astype(jnp.float32) + mlp_out.astype(jnp.float32)).astype(jnp.bfloat16)
    kept = (x_act, normed, query, key_act, value, probs, mixed, hidden, normed2, pre_act, activated)
    return x_next, kept


def layer_backward(d_next, kept, w_query, w_key, w_value, w_proj, w_up, w_down):
    x_act, normed, query, key_act, value, probs, mixed, hidden, normed2, pre_act, activated = kept
    batch, seq_len, heads, head_dim = query.shape
    width = heads * head_dim
    g_down = product("bsf,bsd->fd", activated, d_next)
    d_activated = product("bsd,fd->bsf", d_next, w_down).astype(jnp.bfloat16)
    gelu_pull = jax.vjp(gelu_tanh, pre_act.astype(jnp.float32))[1]
    d_pre = gelu_pull(d_activated.astype(jnp.float32))[0].astype(jnp.bfloat16)
    g_up = product("bsd,bsf->df", normed2, d_pre)
    d_normed2 = product("bsf,df->bsd", d_pre, w_up).astype(jnp.bfloat16)
    hidden_pull = jax.vjp(rms_norm, hidden.astype(jnp.float32))[1]
    d_hidden = (d_next.astype(jnp.float32) + hidden_pull(d_normed2.astype(jnp.float32))[0]).astype(jnp.bfloat16)
    g_proj = product("bsd,bse->de", mixed, d_hidden)
    d_mixed = product("bse,de->bsd", d_hidden, w_proj).astype(jnp.bfloat16).reshape(batch, seq_len, heads, head_dim)
    d_probs = product("bqhd,bkhd->bhqk", d_mixed, value).astype(jnp.bfloat16).astype(jnp.float32)
    d_value = product("bhqk,bqhd->bkhd", probs, d_mixed).astype(jnp.bfloat16).reshape(batch, seq_len, width)
    probs_f32 = probs.astype(jnp.float32)
    row_dot = jnp.sum(d_probs * probs_f32, axis=-1, keepdims=True)
    d_scores = (probs_f32 * (d_probs - row_dot) * head_dim ** -0.5).astype(jnp.bfloat16)
    d_query = product("bhqk,bkhd->bqhd", d_scores, key_act).astype(jnp.bfloat16).reshape(batch, seq_len, width)
    d_key = product("bhqk,bqhd->bkhd", d_scores, query).astype(jnp.bfloat16).reshape(batch, seq_len, width)
    g_query = product("bsd,bse->de", normed, d_query)
    g_key = product("bsd,bse->de", normed, d_key)
    g_value = product("bsd,bse->de", normed, d_value)
    d_normed = (product("bse,de->bsd", d_query, w_query) + product("bse,de->bsd", d_key, w_key)
                + product("bse,de->bsd", d_value, w_value)).astype(jnp.bfloat16)
    input_pull = jax.vjp(rms_norm, x_act.astype(jnp.float32))[1]
    d_input = (d_hidden.astype(jnp.float32) + input_pull(d_normed.astype(jnp.float32))[0]).astype(jnp.bfloat16)
    return d_input, (g_query, g_key, g_value, g_proj), g_up, g_down


def solution(mesh):
    def local_step(x_init, cot_out, w_query, w_key, w_value, w_proj, w_up, w_down):
        heads = x_init.shape[-1] // HEAD_DIM
        layers = w_query.shape[0]
        x_act = x_init
        kept_all = []
        for layer in range(layers):
            x_act, kept = layer_forward(x_act, w_query[layer], w_key[layer], w_value[layer], w_proj[layer], w_up, w_down, heads)
            kept_all.append(kept)
        d_act = cot_out
        g_up = jnp.zeros(w_up.shape, jnp.float32)
        g_down = jnp.zeros(w_down.shape, jnp.float32)
        attn_grads = []
        for layer in reversed(range(layers)):
            d_act, attn_part, up_part, down_part = layer_backward(
                d_act, kept_all[layer], w_query[layer], w_key[layer], w_value[layer], w_proj[layer], w_up, w_down)
            attn_part, up_part, down_part = lax.psum((attn_part, up_part, down_part), "data")
            attn_grads.append(attn_part)
            g_up = g_up + up_part
            g_down = g_down + down_part
        attn_grads = attn_grads[::-1]
        g_query = jnp.stack([part[0] for part in attn_grads])
        g_key = jnp.stack([part[1] for part in attn_grads])
        g_value = jnp.stack([part[2] for part in attn_grads])
        g_proj = jnp.stack([part[3] for part in attn_grads])
        return g_query, g_key, g_value, g_proj, g_up, g_down, d_act

    data_spec = P("data")
    full_spec = P()
    in_specs = (data_spec, data_spec, full_spec, full_spec, full_spec, full_spec, full_spec, full_spec)
    out_specs = (full_spec, full_spec, full_spec, full_spec, full_spec, full_spec, data_spec)
    return jax.shard_map(local_step, mesh=mesh, in_specs=in_specs, out_specs=out_specs, check_vma=False)
```

profile of v0, /device:TPU:0, one launch (start us, length us, event | category | flops | bytes accessed | tf_op | source)
XLA Modules:
  0.0 3790.5 jit_solution(8564740410447731056)
XLA Ops:
  65.7 17.1 fusion.587
  82.9 14.9 divide_convert_fusion.5
  121.2 27.3 convolution_convert_fusion.5
  148.5 34.7 fusion.151
  235.7 17.2 fusion.588
  252.9 14.5 divide_convert_fusion.4
  287.2 27.2 convolution_convert_fusion.4
  314.4 34.5 fusion.159
  401.5 17.2 fusion.589
  418.7 14.5 divide_convert_fusion.3
  453.0 27.1 convolution_convert_fusion.3
  480.1 34.5 fusion.167
  567.1 17.2 fusion.590
  584.3 14.5 divide_convert_fusion.2
  618.6 27.1 convolution_convert_fusion.2
  645.8 34.5 fusion.175
  732.8 17.2 fusion.591
  784.3 27.2 convolution_convert_fusion.1
  811.5 34.5 fusion.183
  898.3 17.2 fusion.592
  949.6 27.7 convolution_convert_fusion
  977.3 57.6 %fusion.20 = bf16[32,128,3072]{2,1,0:T(8,128)(2,1)} fusion(bf16[32,128,3072]{2,1,0:T(8,128)(2,1)} %convolution_convert_fusion, bf16[32,128,768]{2,1,0:T(8,128)(2,1)} %param.9, bf16[3072,768]{1,0:T(8,128)(2,1)} %param.15), kind=kOutput, calls=%fused_computation.56 | convolution fusion | flops 19616759808 | bytes 61341696 | tf_op jit(solution)/shard_map/bsd,fd->bsf/dot_general | solution.py:19
  1034.9 25.0 fusion.142
  1059.9 26.0 fusion.221
  1136.8 23.8 fusion.286
  1160.6 23.4 fusion.287
  1234.2 17.4 fusion.186
  1259.8 31.8 fusion.572
  1291.6 50.0 %fusion.23 = bf16[32,128,3072]{2,1,0:T(8,128)(2,1)} fusion(bf16[32,128,3072]{2,1,0:T(8,128)(2,1)} %convolution_convert_fusion.1, bf16[32,128,768]{2,1,0:T(8,128)(2,1)S(1)} %fusion.119, bf16[3072,768]{1,0:T(8,128)(2,1)S(1)} %bitcast.739), kind=kOutput, calls=%fused_computation.59 | convolution fusion | flops 19616759808 | bytes 61341696 | tf_op jit(solution)/shard_map/bsd,fd->bsf/dot_general | solution.py:19
  1341.7 26.1 fusion.182
  1367.8 25.9 fusion.207
  1446.7 23.8 fusion.284
  1470.5 23.4 fusion.285
  1543.8 17.7 fusion.178
  1569.9 31.7 fusion.575
  1601.6 50.0 %fusion.26 = bf16[32,128,3072]{2,1,0:T(8,128)(2,1)} fusion(bf16[32,128,3072]{2,1,0:T(8,128)(2,1)} %convolution_convert_fusion.2, bf16[32,128,768]{2,1,0:T(8,128)(2,1)S(1)} %fusion.123, bf16[3072,768]{1,0:T(8,128)(2,1)S(1)} %bitcast.741), kind=kOutput, calls=%fused_computation.62 | convolution fusion | flops 19616759808 | bytes 61341696 | tf_op jit(solution)/shard_map/bsd,fd->bsf/dot_general | solution.py:19
  1651.6 26.1 fusion.174
  1677.7 25.9 fusion.210
  1756.4 23.7 fusion.282
  1780.2 23.4 fusion.283
  1853.7 17.7 fusion.170
  1879.7 31.8 fusion.578
  1911.5 50.0 %fusion.29 = bf16[32,128,3072]{2,1,0:T(8,128)(2,1)} fusion(bf16[32,128,3072]{2,1,0:T(8,128)(2,1)} %convolution_convert_fusion.3, bf16[32,128,768]{2,1,0:T(8,128)(2,1)S(1)} %fusion.127, bf16[3072,768]{1,0:T(8,128)(2,1)S(1)} %bitcast.743), kind=kOutput, calls=%fused_computation.65 | convolution fusion | flops 19616759808 | bytes 61341696 | tf_op jit(solution)/shard_map/bsd,fd->bsf/dot_general | solution.py:19
  1961.5 26.1 fusion.166
  1987.6 25.8 fusion.213
  2066.4 23.8 fusion.280
  2090.2 23.4 fusion.281
  2163.7 17.3 fusion.162
  2189.4 31.7 fusion.581
  2221.1 50.0 %fusion.32 = bf16[32,128,3072]{2,1,0:T(8,128)(2,1)} fusion(bf16[32,128,3072]{2,1,0:T(8,128)(2,1)} %convolution_convert_fusion.4, bf16[32,128,768]{2,1,0:T(8,128)(2,1)S(1)} %fusion.131, bf16[3072,768]{1,0:T(8,128)(2,1)S(1)} %bitcast.745), kind=kOutput, calls=%fused_computation.68 | convolution fusion | flops 19616759808 | bytes 61341696 | tf_op jit(solution)/shard_map/bsd,fd->bsf/dot_general | solution.py:19
  2271.2 26.1 fusion.158
  2297.2 25.8 fusion.216
  2376.1 23.8 fusion.278
  2399.9 23.4 fusion.279
  2473.5 17.3 fusion.154
  2499.1 31.7 fusion.584
  2530.9 50.0 %fusion.35 = bf16[32,128,3072]{2,1,0:T(8,128)(2,1)} fusion(bf16[32,128,3072]{2,1,0:T(8,128)(2,1)} %convolution_convert_fusion.5, bf16[32,128,768]{2,1,0:T(8,128)(2,1)S(1)} %fusion.135, bf16[3072,768]{1,0:T(8,128)(2,1)S(1)} %bitcast.747), kind=kOutput, calls=%fused_computation.71 | convolution fusion | flops 19616759808 | bytes 61341696 | tf_op jit(solution)/shard_map/bsd,fd->bsf/dot_general | solution.py:19
  2580.9 26.1 fusion.150
  2660.0 23.6 fusion.276
  2683.6 23.5 fusion.277
  2738.6 38.9 %bitcast_add_fusion = f32[3072,768]{1,0:T(8,128)} fusion(f32[3072,768,1]{1,0,2:T(8,128)} %fusion.584, f32[3072,768,1]{1,0,2:T(8,128)} %fusion.581, f32[3072,768,1]{1,0,2:T(8,128)} %fusion.578, f32[3072,768,1]{1,0,2:T(8,128)} %fusion.575, f32[3072,768,1]{1,0,2:T(8,128)} %fusion.572, bf16[32,128,768]{2,1,0:T(8,128)(2,1)} %param.9, ...), kind=kOutput, calls=%fused_computation.347 | convolution fusion | flops 19464978432 | bytes 88080384 | tf_op jit(solution)/shard_map/bsf,bsd->fd/dot_general | solution.py:19
  2777.4 36.0 bitcast_add_fusion.5
  2834.0 17.4 fusion.146
  2861.8 868.1 %all-reduce.3.cloned.1.call-done = (f32[1,768,768]{2,1,0:T(8,128)}, f32[1,768,768]{2,1,0:T(8,128)}, f32[1,768,768]{2,1,0:T(8,128)}, f32[1,768,768]{2,1,0:T(8,128...) async-done(((f32[1,768,768]{2,1,0:T(8,128)}, ...) | async-done | bytes 75497488 | tf_op jit(solution)/shard_map/psum | solution.py:91
  (527 shorter events, 1194.8 us)
Async XLA Ops:
  7.2 3722.7 %all-reduce.3.cloned.1.call-start = ((), (), s32[]{:S(2)}) async-start(), calls=%async_computation | async-start | bytes 150994944 | tf_op jit(solution)/shard_map/psum | solution.py:91
  11.9 35.9 copy-start.62
  82.9 27.6 slice-start
  110.4 38.1 %slice-start.34 = ((s8[4718592]{0:T(1024)(128)(4,1)}), s8[524288]{0:T(1024)(128)(4,1)S(1)}, s32[]{:S(2)}) async-start(s8[4718592]{0:T(1024)(128)(4,1)} %bitcast.728), calls=%async_computation.35 | async-start | bytes 1048576
  121.2 27.3 copy-start.29
  121.2 27.3 slice-start.35
  275.7 38.7 %slice-start.36 = ((s8[4718592]{0:T(1024)(128)(4,1)}), s8[4194304]{0:T(1024)(128)(4,1)S(1)}, s32[]{:S(2)}) async-start(s8[4718592]{0:T(1024)(128)(4,1)} %bitcast.730), calls=%async_computation.37 | async-start | bytes 8388608
  287.2 27.2 copy-start.67
  287.2 27.2 slice-start.37
  441.5 38.6 %slice-start.38 = ((s8[4718592]{0:T(1024)(128)(4,1)}), s8[4194304]{0:T(1024)(128)(4,1)S(1)}, s32[]{:S(2)}) async-start(s8[4718592]{0:T(1024)(128)(4,1)} %bitcast.732), calls=%async_computation.39 | async-start | bytes 8388608
  453.0 27.1 copy-start.71
  453.0 27.1 slice-start.39
  607.1 38.7 %slice-start.40 = ((s8[4718592]{0:T(1024)(128)(4,1)}), s8[4194304]{0:T(1024)(128)(4,1)S(1)}, s32[]{:S(2)}) async-start(s8[4718592]{0:T(1024)(128)(4,1)} %bitcast.734), calls=%async_computation.41 | async-start | bytes 8388608
  618.6 27.1 copy-start.75
  618.6 27.1 slice-start.41
  772.8 38.7 %slice-start.42 = ((s8[4718592]{0:T(1024)(128)(4,1)}), s8[4194304]{0:T(1024)(128)(4,1)S(1)}, s32[]{:S(2)}) async-start(s8[4718592]{0:T(1024)(128)(4,1)} %bitcast.736), calls=%async_computation.43 | async-start | bytes 8388608
  784.2 27.2 copy-start.79
  784.3 27.2 slice-start.43
  949.6 85.3 %slice-start.32 = ((s8[6291456]{0:T(1024)(128)(4,1)}), s8[2097152]{0:T(1024)(128)(4,1)S(1)}, s32[]{:S(2)}) async-start(s8[6291456]{0:T(1024)(128)(4,1)} %bitcast.726), calls=%async_computation.33 | async-start | bytes 4194304
  977.3 57.6 %slice-start.33 = ((s8[6291456]{0:T(1024)(128)(4,1)}), s8[4194304]{0:T(1024)(128)(4,1)S(1)}, s32[]{:S(2)}) async-start(s8[6291456]{0:T(1024)(128)(4,1)} %bitcast.726), calls=%async_computation.34 | async-start | bytes 8388608
  1059.9 26.0 copy-start.104
  1059.9 26.0 copy-start.32
  1160.6 23.4 copy-start.82
  1184.1 21.6 slice-start.24
  1251.6 40.1 %slice-start.44 = ((s8[4718592]{0:T(1024)(128)(4,1)}), s8[524288]{0:T(1024)(128)(4,1)S(1)}, s32[]{:S(2)}) async-start(s8[4718592]{0:T(1024)(128)(4,1)} %bitcast.738), calls=%async_computation.45 | async-start | bytes 1048576
  1259.8 31.8 slice-start.45
  1291.6 50.1 %copy-start.36 = (bf16[32,128,768]{2,1,0:T(8,128)(2,1)S(1)}, bf16[32,128,768]{2,1,0:T(8,128)(2,1)}, u32[]{:S(2)}) copy-start(bf16[32,128,768]{2,1,0:T(8,128)(2,1)} %get-tuple-element.60) | copy-start | bytes 18874372
  1341.7 26.1 copy-start.80
  1367.8 25.9 copy-start.100
  1470.5 23.4 copy-start.78
  1493.9 21.5 slice-start.22
  1561.5 40.1 %slice-start.46 = ((s8[4718592]{0:T(1024)(128)(4,1)}), s8[524288]{0:T(1024)(128)(4,1)S(1)}, s32[]{:S(2)}) async-start(s8[4718592]{0:T(1024)(128)(4,1)} %bitcast.740), calls=%async_computation.47 | async-start | bytes 1048576
  1569.8 31.7 slice-start.47
  1601.6 50.0 %copy-start.35 = (bf16[32,128,768]{2,1,0:T(8,128)(2,1)S(1)}, bf16[32,128,768]{2,1,0:T(8,128)(2,1)}, u32[]{:S(2)}) copy-start(bf16[32,128,768]{2,1,0:T(8,128)(2,1)} %get-tuple-element.54) | copy-start | bytes 18874372
  1651.6 26.1 copy-start.76
  1677.7 25.9 copy-start.96
  1780.2 23.4 copy-start.74
  1803.6 21.5 slice-start.20
  1825.2 21.2 slice-start.10
  1871.4 40.1 %slice-start.48 = ((s8[4718592]{0:T(1024)(128)(4,1)}), s8[524288]{0:T(1024)(128)(4,1)S(1)}, s32[]{:S(2)}) async-start(s8[4718592]{0:T(1024)(128)(4,1)} %bitcast.742), calls=%async_computation.49 | async-start | bytes 1048576
  1879.7 31.8 slice-start.49
  1911.5 50.0 %copy-start.34 = (bf16[32,128,768]{2,1,0:T(8,128)(2,1)S(1)}, bf16[32,128,768]{2,1,0:T(8,128)(2,1)}, u32[]{:S(2)}) copy-start(bf16[32,128,768]{2,1,0:T(8,128)(2,1)} %get-tuple-element.48) | copy-start | bytes 18874372
  1961.5 26.1 copy-start.72
  1987.6 25.8 copy-start.92
  2090.2 23.4 copy-start.70
  2113.6 21.6 slice-start.18
  2135.2 21.1 slice-start.12
  2181.1 40.0 %slice-start.50 = ((s8[4718592]{0:T(1024)(128)(4,1)}), s8[524288]{0:T(1024)(128)(4,1)S(1)}, s32[]{:S(2)}) async-start(s8[4718592]{0:T(1024)(128)(4,1)} %bitcast.744), calls=%async_computation.51 | async-start | bytes 1048576
  2189.4 31.7 slice-start.51
  2221.1 50.0 %copy-start.33 = (bf16[32,128,768]{2,1,0:T(8,128)(2,1)S(1)}, bf16[32,128,768]{2,1,0:T(8,128)(2,1)}, u32[]{:S(2)}) copy-start(bf16[32,128,768]{2,1,0:T(8,128)(2,1)} %get-tuple-element.42) | copy-start | bytes 18874372
  2271.2 26.1 copy-start.68
  2297.2 25.8 copy-start.88
  2399.9 23.4 copy-start.66
  2423.3 21.7 slice-start.16
  2444.9 21.1 slice-start.14
  2490.8 40.0 %slice-start.52 = ((s8[4718592]{0:T(1024)(128)(4,1)}), s8[524288]{0:T(1024)(128)(4,1)S(1)}, s32[]{:S(2)}) async-start(s8[4718592]{0:T(1024)(128)(4,1)} %bitcast.746), calls=%async_computation.53 | async-start | bytes 1048576
  2499.1 31.7 slice-start.53
  2530.9 50.0 %copy-start.11 = (bf16[32,128,768]{2,1,0:T(8,128)(2,1)S(1)}, bf16[32,128,768]{2,1,0:T(8,128)(2,1)}, u32[]{:S(2)}) copy-start(bf16[32,128,768]{2,1,0:T(8,128)(2,1)} %get-tuple-element.36) | copy-start | bytes 18874372
  2580.9 26.1 copy-start.84
  2580.9 26.1 copy-start.30
  2683.6 23.5 copy-start.63
  2707.1 23.8 slice-start.2
  2707.2 23.7 slice-start.4
  2738.6 38.9 %copy-start.31 = (f32[32,128]{1,0:T(8,128)S(1)}, f32[32,128]{1,0:T(8,128)}, u32[]{:S(2)}) copy-start(f32[32,128]{1,0:T(8,128)} %copy-done.29) | copy-start | bytes 49156
  (101 other events, 1043.2 us)
Sparse Core Ops, SparseCore 0:
  2813.5 916.3 all-reduce.2
where the time goes:
time: 3800 us; the launch traced here: 3790 us
  matrix products  2460 us (65%)
  waiting for transfers between devices  868 us (23%)
  local copies, waits for them, and re-layouts  266 us (7%)
  other arithmetic  179 us (5%)
    dot_general x137, matrix products, product(): return jnp.einsum(subscripts, lhs, rhs, preferred_element_type=jnp.float32)  2360 us
    psum x1, waiting for transfers between devices, local_step(): lax.psum((attn_part, up_part, down_part), 'data')  868 us
    sub x6, matrix products, layer_forward(): probs = jax.nn.softmax(scores, axis=-1).astype(jnp.bfloat16)  103 us
    convert_element_type x6, other arithmetic, layer_forward(): probs = jax.nn.softmax(scores, axis=-1).astype(jnp.bfloat16)  87.5 us
  transfers between devices with their start and end apart: 1, of which 1 were waited for; matrix products, arithmetic and copies ran while one was open for 1% of the time, Pallas kernels for 0%

commit v1 on v0

v1 whole, which is shorter than its diff:
```python
import functools

import jax
import jax.numpy as jnp
from jax import lax
from jax.experimental import pallas as pl
from jax.experimental.pallas import tpu as pltpu
from jax.sharding import PartitionSpec as P

EPS = 1e-6
HEAD_DIM = 64
BF = jnp.bfloat16
F32 = jnp.float32
SEQ = 128
PAIR = 2 * HEAD_DIM
SCALE = HEAD_DIM ** -0.5
LOG2E = 1.4426950408889634
GC = 0.7978845608028654
GA = 0.044715


def mm(a, b, ca=1, cb=0):
    return lax.dot_general(a, b, (((ca,), (cb,)), ((), ())), preferred_element_type=F32)


def inv_rms(v):
    return lax.rsqrt(jnp.mean(v * v, axis=-1, keepdims=True) + EPS)


def stack_heads(val):
    lane = lax.broadcasted_iota(jnp.int32, val.shape, 1)
    zero = jnp.zeros_like(val)
    return jnp.concatenate([jnp.where(lane < HEAD_DIM, val, zero), jnp.where(lane < HEAD_DIM, zero, val)], axis=0)


def rows_of(val):
    return jnp.concatenate([val[:, :SEQ], val[:, SEQ:]], axis=0)


def gelu(x):
    t = jnp.tanh(x * (GC + (GC * GA) * (x * x)))
    h = 0.5 * x
    return h + h * t


def fwd_body(x_ref, wq, wk, wv, wo, w1, w2, xs_o, q_o, k_o, v_o, p_o, mix_o, hid_o, n2_o, pre_o, act_o, xbuf, *, layers, tb):
    layer = pl.program_id(0)
    rows = pl.ds(pl.multiple_of(pl.program_id(1) * tb, tb), tb)
    pairs = q_o.shape[-1] // PAIR

    @pl.when(layer == 0)
    def _():
        xbuf[rows, :] = x_ref[...]

    x_bf = xbuf[rows, :]
    xs_o[0] = x_bf
    x = x_bf.astype(F32)
    normed = (x * inv_rms(x)).astype(BF)
    q_o[0] = mm(normed, wq[0]).astype(BF)
    k_o[0] = mm(normed, wk[0]).astype(BF)
    v_o[0] = mm(normed, wv[0]).astype(BF)

    def attend(s, carry):
        sl = pl.ds(pl.multiple_of(s * SEQ, SEQ), SEQ)
        for p in range(pairs):
            lanes = slice(p * PAIR, (p + 1) * PAIR)
            st = mm(k_o[0, sl, lanes], stack_heads(q_o[0, sl, lanes]), 1, 1)
            top = jnp.max(st, axis=0, keepdims=True)
            e = jnp.exp2((st - top) * (SCALE * LOG2E))
            prob = (e * (1.0 / jnp.sum(e, axis=0, keepdims=True))).astype(BF)
            p_o[0, pl.ds(pl.multiple_of((s * pairs + p) * SEQ, SEQ), SEQ), :] = prob
            mix_o[0, sl, lanes] = mm(rows_of(prob), stack_heads(v_o[0, sl, lanes]), 0, 0).astype(BF)
        return carry

    lax.fori_loop(0, tb // SEQ, attend, 0)
    hid = (x + mm(mix_o[0], wo[0]).astype(BF).astype(F32)).astype(BF)
    hid_o[0] = hid
    h = hid.astype(F32)
    n2 = (h * inv_rms(h)).astype(BF)
    n2_o[0] = n2
    ff = w1.shape[1]
    step = 768
    for j in range(ff // step):
        cols = slice(j * step, (j + 1) * step)
        pre = mm(n2, w1[:, cols]).astype(BF)
        pre_o[0, :, cols] = pre
        act_o[0, :, cols] = gelu(pre.astype(F32)).astype(BF)

    @pl.when(layer < layers - 1)
    def _():
        out = mm(act_o[0], w2[...]).astype(BF).astype(F32)
        xbuf[rows, :] = (hid_o[0].astype(F32) + out).astype(BF)


def forward(x, wq, wk, wv, wo, w1, w2, tb=512):
    layers, d, _ = wq.shape
    ff = w1.shape[1]
    t = x.shape[0]
    nb = t // tb
    prow = (tb // SEQ) * (d // PAIR) * SEQ
    wspec = pl.BlockSpec((1, d, d), lambda l, b: (l, 0, 0))
    once = pl.Buffered(1)

    def tok(w):
        return pl.BlockSpec((1, tb, w), lambda l, b: (l, b, 0))

    def sds(w):
        return jax.ShapeDtypeStruct((layers, t, w), BF)


    return pl.pallas_call(
        functools.partial(fwd_body, layers=layers, tb=tb),
        grid=(layers, nb),
        in_specs=[pl.BlockSpec((tb, d), lambda l, b: (jnp.where(l == 0, b, nb - 1), 0)), wspec, wspec, wspec, wspec,
                  pl.BlockSpec((d, ff), lambda l, b: (0, 0), pipeline_mode=once),
                  pl.BlockSpec((ff, d), lambda l, b: (0, 0), pipeline_mode=once)],
        out_specs=[tok(d), tok(d), tok(d), tok(d), pl.BlockSpec((1, prow, 2 * SEQ), lambda l, b: (l, b, 0)),
                   tok(d), tok(d), tok(d), tok(ff), tok(ff)],
        out_shape=[sds(d), sds(d), sds(d), sds(d), jax.ShapeDtypeStruct((layers, nb * prow, 2 * SEQ), BF),
                   sds(d), sds(d), sds(d), sds(ff), sds(ff)],
        scratch_shapes=[pltpu.VMEM((t, d), BF)],
        compiler_params=pltpu.CompilerParams(dimension_semantics=("arbitrary", "arbitrary"), vmem_limit_bytes=63 * 1024 * 1024),
        name="fwd_stack",
    )(x, wq, wk, wv, wo, w1, w2)


def rms_pull(v, dy):
    r = inv_rms(v)
    return dy * r - v * (r * r * r * jnp.mean(v * dy, axis=-1, keepdims=True))


def gelu_pull(x, d):
    sq = x * x
    t = jnp.tanh(x * (GC + (GC * GA) * sq))
    return d * (0.5 + 0.5 * t + (0.5 * x) * (1.0 - t * t) * (GC + (3.0 * GC * GA) * sq))


def bwd_body(dn_ref, x_ref, q_ref, k_ref, v_ref, p_ref, mix_ref, hid_ref, pre_ref, wq, wk, wv, wo, w1, w2,
             dx_o, keep_o, dpre_o, g_o, dmix, dq, dk, dv):
    @pl.when(pl.program_id(0) == 0)
    def _():
        g_o[...] = jnp.zeros_like(g_o)

    tb, d = dx_o.shape
    pairs = d // PAIR
    dn = dn_ref[...]
    keep_o[0] = dn
    ff = w1.shape[1]
    step = 768
    for j in range(ff // step):
        cols = slice(j * step, (j + 1) * step)
        d_act = mm(dn, w2[cols, :], 1, 1).astype(BF).astype(F32)
        dpre_o[0, :, cols] = gelu_pull(pre_ref[0, :, cols].astype(F32), d_act).astype(BF)
    d_n2 = mm(dpre_o[0], w1[...], 1, 1).astype(BF).astype(F32)
    dh = (dn.astype(F32) + rms_pull(hid_ref[0].astype(F32), d_n2)).astype(BF)
    dmix[...] = mm(dh, wo[0], 1, 1).astype(BF)
    g_o[3] += mm(mix_ref[0], dh, 0, 0)

    def attend(s, carry):
        sl = pl.ds(pl.multiple_of(s * SEQ, SEQ), SEQ)
        for p in range(pairs):
            lanes = slice(p * PAIR, (p + 1) * PAIR)
            prob = p_ref[0, pl.ds(pl.multiple_of((s * pairs + p) * SEQ, SEQ), SEQ), :]
            d_mixed = stack_heads(dmix[sl, lanes])
            d_prob = mm(v_ref[0, sl, lanes], d_mixed, 1, 1).astype(BF).astype(F32)
            dv[sl, lanes] = mm(prob, d_mixed, 1, 0).astype(BF)
            prob = prob.astype(F32)
            row = jnp.sum(d_prob * prob, axis=0, keepdims=True)
            d_st = (prob * (d_prob - row) * SCALE).astype(BF)
            dk[sl, lanes] = mm(d_st, stack_heads(q_ref[0, sl, lanes]), 1, 0).astype(BF)
            dq[sl, lanes] = mm(rows_of(d_st), stack_heads(k_ref[0, sl, lanes]), 0, 0).astype(BF)
        return carry

    lax.fori_loop(0, tb // SEQ, attend, 0)
    x = x_ref[0].astype(F32)
    normed = (x * inv_rms(x)).astype(BF)
    g_o[0] += mm(normed, dq[...], 0, 0)
    g_o[1] += mm(normed, dk[...], 0, 0)
    g_o[2] += mm(normed, dv[...], 0, 0)
    d_n1 = (mm(dq[...], wq[0], 1, 1) + mm(dk[...], wk[0], 1, 1) + mm(dv[...], wv[0], 1, 1)).astype(BF).astype(F32)
    dx_o[...] = (dh.astype(F32) + rms_pull(x, d_n1)).astype(BF)


def backward(layer, d_next, xs, q, k, v, p, mix, hid, pre, wq, wk, wv, wo, w1, w2, tb=256):
    layers, d, _ = wq.shape
    ff = w1.shape[1]
    t = d_next.shape[0]
    prow = (tb // SEQ) * (d // PAIR) * SEQ
    once = pl.Buffered(1)
    wspec = pl.BlockSpec((1, d, d), lambda b: (layer, 0, 0), pipeline_mode=once)
    flat = pl.BlockSpec((tb, d), lambda b: (b, 0))

    def tok(w):
        return pl.BlockSpec((1, tb, w), lambda b: (layer, b, 0))

    return pl.pallas_call(
        bwd_body,
        grid=(t // tb,),
        in_specs=[flat, tok(d), tok(d), tok(d), tok(d), pl.BlockSpec((1, prow, 2 * SEQ), lambda b: (layer, b, 0)),
                  tok(d), tok(d), tok(ff), wspec, wspec, wspec, wspec,
                  pl.BlockSpec((d, ff), lambda b: (0, 0), pipeline_mode=once),
                  pl.BlockSpec((ff, d), lambda b: (0, 0), pipeline_mode=once)],
        out_specs=[flat, tok(d), tok(ff), pl.BlockSpec((4, d, d), lambda b: (0, 0, 0), pipeline_mode=once)],
        out_shape=[jax.ShapeDtypeStruct((t, d), BF), jax.ShapeDtypeStruct(xs.shape, BF), jax.ShapeDtypeStruct(pre.shape, BF),
                   jax.ShapeDtypeStruct((4, d, d), F32)],
        input_output_aliases={1: 1, 8: 2},
        scratch_shapes=[pltpu.VMEM((tb, d), BF)] * 4,
        cost_estimate=pl.CostEstimate(flops=80 * 10 ** 9, transcendentals=0, bytes_accessed=150 * 10 ** 6),
        compiler_params=pltpu.CompilerParams(dimension_semantics=("arbitrary",), vmem_limit_bytes=63 * 1024 * 1024),
        name="bwd_layer",
    )(d_next, xs, q, k, v, p, mix, hid, pre, wq, wk, wv, wo, w1, w2)


def local_step(x_init, cot_out, w_query, w_key, w_value, w_proj, w_up, w_down):
    layers, width, _ = w_query.shape
    x = x_init.reshape(-1, width)
    weights = (w_query, w_key, w_value, w_proj, w_up, w_down)
    xs, q, k, v, p, mix, hid, n2, pre, act = forward(x, *weights)
    d_act = cot_out.reshape(-1, width)
    sums = [None] * layers
    last = None
    for layer in reversed(range(layers)):
        d_act, xs, pre, part = backward(layer, d_act, xs, q, k, v, p, mix, hid, pre, *weights)
        if last is not None:
            part, last = lax.optimization_barrier((part, last))
            sums[layer + 1] = last
        last = lax.psum(part, "data")
    tall = lambda a: a.reshape(-1, a.shape[-1])
    g_up = mm(tall(n2), tall(pre), 0, 0)
    g_up, last = lax.optimization_barrier((g_up, last))
    sums[0] = last
    g_up = lax.psum(g_up, "data")
    g_down = mm(tall(act), tall(xs), 0, 0)
    g_down, g_up = lax.optimization_barrier((g_down, g_up))
    g_down = lax.psum(g_down, "data")
    attn = [jnp.stack([part[i] for part in sums]) for i in range(4)]
    return (*attn, g_up, g_down, d_act.reshape(x_init.shape))


def solution(mesh):
    data_spec = P("data")
    full_spec = P()
    in_specs = (data_spec, data_spec) + (full_spec,) * 6
    out_specs = (full_spec,) * 6 + (data_spec,)
    return jax.shard_map(local_step, mesh=mesh, in_specs=in_specs, out_specs=out_specs, check_vma=False)
```

time: 3800 us -> 2120 us (0.56)
  matrix products: 2460 us -> 263 us
  Pallas kernels: 0 us -> 1700 us
  waiting for transfers between devices: 868 us -> 90.1 us
  local copies, waits for them, and re-layouts: 266 us -> 51.7 us
  other arithmetic: 179 us -> 0.01 us
    dot_general x137 -> x2, matrix products: 2360 us -> 263 us  [mm(): lax.dot_general(a, b, (((ca,), (cb,)), ((), ())), preferred_element_type=...]
    pallas_call x0 -> x7, Pallas kernels: none -> 1700 us  [the longest x6 1070 us: backward(): pl.pallas_call(bwd_body, grid=(t // tb,), in_specs=[flat, tok(d), tok(d),...]
    psum x1 -> x8, waiting for transfers between devices: 868 us -> 89.9 us  [the longest x1 89.8 us: local_step(): g_down = lax.psum(g_down, 'data')]
    convert_element_type x24 -> x0, local copies, waits for them, and re-layouts: 208 us -> none  [the longest x6 51.9 us: layer_forward(): product('bsd,de->bse', normed, w_query).astype(jnp.bfloat16)]
    convert_element_type x18 -> x0, other arithmetic: 175 us -> none  [the longest x6 87.5 us: layer_forward(): probs = jax.nn.softmax(scores, axis=-1).astype(jnp.bfloat16)]
    sub x6 -> x0, matrix products: 103 us -> none  [layer_forward(): probs = jax.nn.softmax(scores, axis=-1).astype(jnp.bfloat16)]
  transfers between devices with their start and end apart: 1 -> 8, of which waited for: 1 -> 1; matrix products, arithmetic and copies ran while one was open for 1% -> 14% of each run, Pallas kernels for 0% -> 42%
where the time goes in v1:
time: 2120 us
  Pallas kernels  1700 us (80%)
  matrix products  263 us (12%)
  waiting for transfers between devices  90.1 us (4%)
  local copies, waits for them, and re-layouts  51.7 us (2%)
    pallas_call x6, Pallas kernels, backward(): pl.pallas_call(bwd_body, grid=(t // tb,), in_specs=[flat, tok(d), tok(d),...  1070 us
    pallas_call x1, Pallas kernels, forward(): pl.pallas_call(functools.partial(fwd_body, layers=layers, tb=tb), grid=(l...  630 us
    dot_general x2, matrix products, mm(): lax.dot_general(a, b, (((ca,), (cb,)), ((), ())), preferred_element_type=...  263 us
    psum x1, waiting for transfers between devices, local_step(): g_down = lax.psum(g_down, 'data')  89.8 us
    unnamed x37, local copies, waits for them, and re-layouts  47.9 us
  transfers between devices with their start and end apart: 8, of which 1 were waited for; matrix products, arithmetic and copies ran while one was open for 14% of the time, Pallas kernels for 42%

profile of v1, /device:TPU:0, one launch (start us, length us, event | category | flops | bytes accessed | tf_op | source)
XLA Modules:
  0.0 2116.0 jit_solution(5840518071580335586)
XLA Ops:
  7.2 0.0 all-reduce.9.cloned.1.call-start
  7.2 630.1 %fwd_stack.1 = (bf16[6,4096,768]{2,1,0:T(8,128)(2,1)}, bf16[6,4096,768]{2,1,0:T(8,128)(2,1)}, bf16[6,4096,768]{2,1,0:T(8,128)(2,1)}, bf16[6,4096,768]{2,1,0:T(8,...) custom-call(bf16[4096,768]{1,0:T(8,128)(2,1)} %bitcast.22, ...), custom_call_target="tpu_custom_call" | custom-call | tf_op jit(solution)/shard_map/fwd_stack/pallas_call | solution.py:111
  637.3 177.7 %bwd_layer.6 = (bf16[4096,768]{1,0:T(8,128)(2,1)}, bf16[6,4096,768]{2,1,0:T(8,128)(2,1)}, bf16[6,4096,3072]{2,1,0:T(8,128)(2,1)}, f32[4,768,768]{2,1,0:T(8,128)}) custom-call(bf16[4096,768]{1,0:T(8,128)(2,1)} %bitcast.21, bf16[6,4096,768]{2,1,0:T(8,128)(2,1)} %get-tuple-element.56.x_ref, ...), custom_call_target="tpu_custom_call", output_to_operand_aliasing={{1}: (1, {}), {2}: (8, {})} | custom-call | flops 80000000000 | bytes 150000000 | tf_op jit(solution)/shard_map/bwd_layer/pallas_call | solution.py:196
  815.0 0.0 all-reduce.9.cloned.1.call-update
  815.1 0.0 all-reduce.11.cloned.1.call-start
  815.1 177.4 %bwd_layer.7 = (bf16[4096,768]{1,0:T(8,128)(2,1)}, bf16[6,4096,768]{2,1,0:T(8,128)(2,1)}, bf16[6,4096,3072]{2,1,0:T(8,128)(2,1)}, f32[4,768,768]{2,1,0:T(8,128)}) custom-call(bf16[4096,768]{1,0:T(8,128)(2,1)} %get-tuple-element.64.dn_ref, bf16[6,4096,768]{2,1,0:T(8,128)(2,1)} %get-tuple-element.65.x_ref, ...), custom_call_target="tpu_custom_call", output_to_operand_aliasing={{1}: (1, {}), {2}: (8, {})} | custom-call | flops 80000000000 | bytes 150000000 | tf_op jit(solution)/shard_map/bwd_layer/pallas_call | solution.py:196
  992.5 0.0 all-reduce.9.cloned.1.call-done
  992.6 0.0 all-reduce.11.cloned.1.call-update
  992.6 0.0 all-reduce.13.cloned.1.call-start
  992.6 177.7 %bwd_layer.8 = (bf16[4096,768]{1,0:T(8,128)(2,1)}, bf16[6,4096,768]{2,1,0:T(8,128)(2,1)}, bf16[6,4096,3072]{2,1,0:T(8,128)(2,1)}, f32[4,768,768]{2,1,0:T(8,128)}) custom-call(bf16[4096,768]{1,0:T(8,128)(2,1)} %get-tuple-element.67.dn_ref, bf16[6,4096,768]{2,1,0:T(8,128)(2,1)} %get-tuple-element.68.x_ref, ...), custom_call_target="tpu_custom_call", output_to_operand_aliasing={{1}: (1, {}), {2}: (8, {})} | custom-call | flops 80000000000 | bytes 150000000 | tf_op jit(solution)/shard_map/bwd_layer/pallas_call | solution.py:196
  1170.4 0.0 all-reduce.11.cloned.1.call-done
  1170.4 0.0 all-reduce.13.cloned.1.call-update
  1170.4 0.0 all-reduce.15.cloned.1.call-start
  1170.5 177.6 %bwd_layer.9 = (bf16[4096,768]{1,0:T(8,128)(2,1)}, bf16[6,4096,768]{2,1,0:T(8,128)(2,1)}, bf16[6,4096,3072]{2,1,0:T(8,128)(2,1)}, f32[4,768,768]{2,1,0:T(8,128)}) custom-call(bf16[4096,768]{1,0:T(8,128)(2,1)} %get-tuple-element.70.dn_ref, bf16[6,4096,768]{2,1,0:T(8,128)(2,1)} %get-tuple-element.71.x_ref, ...), custom_call_target="tpu_custom_call", output_to_operand_aliasing={{1}: (1, {}), {2}: (8, {})} | custom-call | flops 80000000000 | bytes 150000000 | tf_op jit(solution)/shard_map/bwd_layer/pallas_call | solution.py:196
  1348.1 0.0 all-reduce.13.cloned.1.call-done
  1348.1 0.0 all-reduce.15.cloned.1.call-update
  1348.1 0.0 all-reduce.17.cloned.1.call-start
  1348.2 177.8 %bwd_layer.10 = (bf16[4096,768]{1,0:T(8,128)(2,1)}, bf16[6,4096,768]{2,1,0:T(8,128)(2,1)}, bf16[6,4096,3072]{2,1,0:T(8,128)(2,1)}, f32[4,768,768]{2,1,0:T(8,128)}) custom-call(bf16[4096,768]{1,0:T(8,128)(2,1)} %get-tuple-element.73.dn_ref, bf16[6,4096,768]{2,1,0:T(8,128)(2,1)} %get-tuple-element.74.x_ref, ...), custom_call_target="tpu_custom_call", output_to_operand_aliasing={{1}: (1, {}), {2}: (8, {})} | custom-call | flops 80000000000 | bytes 150000000 | tf_op jit(solution)/shard_map/bwd_layer/pallas_call | solution.py:196
  1525.9 0.0 all-reduce.15.cloned.1.call-done
  1526.0 0.0 all-reduce.17.cloned.1.call-update
  1526.0 0.0 all-reduce.19.cloned.1.call-start
  1526.0 177.7 %bwd_layer.11 = (bf16[4096,768]{1,0:T(8,128)(2,1)}, bf16[6,4096,768]{2,1,0:T(8,128)(2,1)}, bf16[6,4096,3072]{2,1,0:T(8,128)(2,1)}, f32[4,768,768]{2,1,0:T(8,128)}) custom-call(bf16[4096,768]{1,0:T(8,128)(2,1)} %get-tuple-element.76.dn_ref, bf16[6,4096,768]{2,1,0:T(8,128)(2,1)} %get-tuple-element.77.x_ref, ...), custom_call_target="tpu_custom_call", output_to_operand_aliasing={{1}: (1, {}), {2}: (8, {})} | custom-call | flops 80000000000 | bytes 150000000 | tf_op jit(solution)/shard_map/bwd_layer/pallas_call | solution.py:196
  1703.7 0.0 all-reduce.17.cloned.1.call-done
  1703.7 0.0 all-reduce.19.cloned.1.call-update
  1703.8 0.0 all-reduce.21.cloned.1.call-start
  1703.8 129.6 %convolution_bitcast_fusion.1 = f32[768,3072]{1,0:T(8,128)} fusion(bf16[6,4096,768]{2,1,0:T(8,128)(2,1)} %get-tuple-element.55, bf16[6,4096,3072]{2,1,0:T(8,128)(2,1)} %get-tuple-element.79), kind=kOutput, calls=%fused_computation.1 | convolution fusion | flops 115964116992 | bytes 198180864 | tf_op jit(solution)/shard_map/dot_general | solution.py:23
  1833.4 0.0 all-reduce.19.cloned.1.call-done
  1833.4 0.0 all-reduce.21.cloned.1.call-update
  1833.4 0.0 all-reduce.23.cloned.1.call-start
  1833.5 133.6 %convolution_bitcast_fusion = f32[3072,768]{1,0:T(8,128)} fusion(bf16[6,4096,3072]{2,1,0:T(8,128)(2,1)} %get-tuple-element.97, bf16[6,4096,768]{2,1,0:T(8,128)(2,1)} %get-tuple-element.98), kind=kOutput, calls=%fused_computation | convolution fusion | flops 115964116992 | bytes 198180864 | tf_op jit(solution)/shard_map/dot_general | solution.py:23
  1967.0 0.0 all-reduce.21.cloned.1.call-done
  1967.1 0.0 all-reduce.23.cloned.1.call-update
  1967.1 7.6 slice_dynamic-update-slice_fusion.5
  1974.7 0.0 slice-start.9
  1974.7 0.0 slice-start.10
  1974.7 0.0 slice-start.11
  1974.7 8.7 slice_dynamic-update-slice_fusion.4
  1983.4 0.0 slice-start.6
  1983.4 0.0 slice-done.9
  1983.4 0.3 slice-done.10
  1983.6 0.7 slice-done.11
  1984.4 0.0 slice-start.7
  1984.4 0.0 slice-start.8
  1984.4 4.8 slice_dynamic-update-slice_fusion.3
  1989.2 0.0 slice-start.3
  1989.2 0.0 slice-done.6
  1989.2 0.9 slice-done.7
  1990.1 0.4 slice-done.8
  1990.5 0.0 slice-start.4
  1990.5 4.8 slice_dynamic-update-slice_fusion.2
  1995.3 0.0 slice-done.3
  1995.3 0.4 slice-done.4
  1995.7 0.8 slice-done.5
  1996.5 4.8 slice_dynamic-update-slice_fusion.1
  2001.3 0.0 slice-done
  2001.3 0.3 slice-done.1
  2001.6 0.9 slice-done.2
  2002.5 3.8 slice_dynamic-update-slice_fusion
  2006.3 89.8 %all-reduce.23.cloned.1.call-done = f32[3072,768]{1,0:T(8,128)} async-done(((f32[3072,768]{1,0:T(8,128)}), f32[3072,768]{1,0:T(8,128)}) %all-reduce.23.cloned.1.call-update) | async-done | bytes 9437200 | tf_op jit(solution)/shard_map/psum | solution.py:235
  2096.1 8.8 copy.71
  2104.9 0.0 slice-done.12
  2104.9 0.0 slice-done.13
  2104.9 0.0 slice-done.14
  2104.9 3.7 copy.72
  (12 shorter events, 0.0 us)
Async XLA Ops:
  7.2 985.4 %all-reduce.9.cloned.1.call-start = ((), (), s32[]{:S(2)}) async-start(), calls=%async_computation | async-start | bytes 18874368 | tf_op jit(solution)/shard_map/psum | solution.py:227
  815.1 355.3 %all-reduce.11.cloned.1.call-start = ((), (), s32[]{:S(2)}) async-start(), calls=%async_computation.1 | async-start | bytes 18874368 | tf_op jit(solution)/shard_map/psum | solution.py:227
  992.6 355.5 %all-reduce.13.cloned.1.call-start = ((), (), s32[]{:S(2)}) async-start(), calls=%async_computation.2 | async-start | bytes 18874368 | tf_op jit(solution)/shard_map/psum | solution.py:227
  1170.4 355.6 %all-reduce.15.cloned.1.call-start = ((), (), s32[]{:S(2)}) async-start(), calls=%async_computation.3 | async-start | bytes 18874368 | tf_op jit(solution)/shard_map/psum | solution.py:227
  1348.1 355.6 %all-reduce.17.cloned.1.call-start = ((), (), s32[]{:S(2)}) async-start(), calls=%async_computation.4 | async-start | bytes 18874368 | tf_op jit(solution)/shard_map/psum | solution.py:227
  1526.0 307.4 %all-reduce.19.cloned.1.call-start = ((), (), s32[]{:S(2)}) async-start(), calls=%async_computation.5 | async-start | bytes 18874368 | tf_op jit(solution)/shard_map/psum | solution.py:227
  1703.8 263.3 %all-reduce.21.cloned.1.call-start = ((), (), s32[]{:S(2)}) async-start(), calls=%async_computation.6 | async-start | bytes 18874368 | tf_op jit(solution)/shard_map/psum | solution.py:232
  1833.4 262.7 %all-reduce.23.cloned.1.call-start = ((), (), s32[]{:S(2)}) async-start(), calls=%async_computation.7 | async-start | bytes 18874368 | tf_op jit(solution)/shard_map/psum | solution.py:235
  1974.7 8.7 slice-start.9
  1974.7 9.0 slice-start.10
  1974.7 9.7 slice-start.11
  1983.4 5.8 slice-start.6
  1984.4 5.7 slice-start.7
  1984.4 6.1 slice-start.8
  1989.2 6.1 slice-start.3
  1990.5 5.2 slice-start.4
  1990.5 6.0 slice-start.5
  1995.3 6.0 slice-start
  1996.5 5.1 slice-start.1
  1996.5 6.0 slice-start.2
  2096.1 8.8 slice-start.12
  2096.1 8.8 slice-start.13
  2096.1 8.8 slice-start.14
Sparse Core Ops, SparseCore 0:
  815.2 128.8 all-reduce.8
  992.7 128.9 all-reduce.10
  1170.5 128.9 all-reduce.12
  1348.2 128.8 all-reduce.14
  1526.1 128.9 all-reduce.16
  1703.9 128.8 all-reduce.18
  1836.8 126.1 all-reduce.20
  1967.2 128.8 all-reduce.22

commit v2 on v1

v2 whole, which is shorter than its diff:
```python
import functools

import jax
import jax.numpy as jnp
from jax import lax
from jax.experimental import pallas as pl
from jax.experimental.pallas import tpu as pltpu
from jax.sharding import PartitionSpec as P

EPS = 1e-6
HEAD_DIM = 64
BF = jnp.bfloat16
F32 = jnp.float32
SEQ = 128
PAIR = 2 * HEAD_DIM
SCALE = HEAD_DIM ** -0.5
LOG2E = 1.4426950408889634
GC = 0.7978845608028654
GA = 0.044715
FWD_CHUNK = 512
BWD_CHUNK = 768


def mm(a, b, ca=1, cb=0):
    return lax.dot_general(a, b, (((ca,), (cb,)), ((), ())), preferred_element_type=F32)


def inv_rms(v):
    return lax.rsqrt(jnp.mean(v * v, axis=-1, keepdims=True) + EPS)


def stack_heads(val):
    lane = lax.broadcasted_iota(jnp.int32, val.shape, 1)
    zero = jnp.zeros_like(val)
    return jnp.concatenate([jnp.where(lane < HEAD_DIM, val, zero), jnp.where(lane < HEAD_DIM, zero, val)], axis=0)


def rows_of(val):
    return jnp.concatenate([val[:, :SEQ], val[:, SEQ:]], axis=0)


def gelu(x):
    t = jnp.tanh(x * (GC + (GC * GA) * (x * x)))
    h = 0.5 * x
    return h + h * t


def fwd_body(x_ref, wq, wk, wv, wo, w1, w2, xs_o, q_o, k_o, v_o, p_o, mix_o, hid_o, n2_o, pre_o, act_o, xbuf, mixbuf, *, layers, nb, tb):
    s = pl.program_id(0)
    cur = jnp.minimum(s, layers * nb - 1)
    old = jnp.maximum(s - 1, 0)
    rows = pl.ds(pl.multiple_of((cur % nb) * tb, tb), tb)
    rows_old = pl.ds(pl.multiple_of((old % nb) * tb, tb), tb)
    pairs = q_o.shape[-1] // PAIR

    @pl.when(s < nb)
    def _():
        xbuf[rows, :] = x_ref[...]

    @pl.when(s == 0)
    def _():
        mixbuf[...] = jnp.zeros_like(mixbuf)

    hid = (xbuf[rows_old, :].astype(F32) + mm(mixbuf[...], wo[0]).astype(BF).astype(F32)).astype(BF)
    hid_o[0] = hid
    x_bf = xbuf[rows, :]
    xs_o[0] = x_bf
    x = x_bf.astype(F32)
    normed = (x * inv_rms(x)).astype(BF)
    q_o[0] = mm(normed, wq[0]).astype(BF)
    k_o[0] = mm(normed, wk[0]).astype(BF)
    v_o[0] = mm(normed, wv[0]).astype(BF)
    h = hid.astype(F32)
    n2_o[0] = (h * inv_rms(h)).astype(BF)

    units = [(i, p) for i in range(tb // SEQ) for p in range(pairs)]
    ff = w1.shape[1]
    step = FWD_CHUNK
    chunks = ff // step
    each = -(-len(units) // chunks)

    def score(i, p):
        lanes = slice(p * PAIR, (p + 1) * PAIR)
        sl = slice(i * SEQ, (i + 1) * SEQ)
        return mm(k_o[0, sl, lanes], stack_heads(q_o[0, sl, lanes]), 1, 1)

    def soft(i, p, st):
        top = jnp.max(st, axis=0, keepdims=True)
        e = jnp.exp2((st - top) * (SCALE * LOG2E))
        prob = (e * (1.0 / jnp.sum(e, axis=0, keepdims=True))).astype(BF)
        at = (i * pairs + p) * SEQ
        p_o[0, at:at + SEQ, :] = prob
        return prob

    def mixed(i, p, prob):
        lanes = slice(p * PAIR, (p + 1) * PAIR)
        sl = slice(i * SEQ, (i + 1) * SEQ)
        val = mm(rows_of(prob), stack_heads(v_o[0, sl, lanes]), 0, 0).astype(BF)
        mix_o[0, sl, lanes] = val
        mixbuf[sl, lanes] = val

    ready = []
    for j in range(chunks):
        group = units[j * each:(j + 1) * each]
        scores = [score(*u) for u in group]
        for u, prob in ready:
            mixed(*u, prob)
        cols = slice(j * step, (j + 1) * step)
        pre = mm(n2_o[0], w1[:, cols]).astype(BF)
        pre_o[0, :, cols] = pre
        ready = [(u, soft(*u, st)) for u, st in zip(group, scores)]
        act_o[0, :, cols] = gelu(pre.astype(F32)).astype(BF)
    for u, prob in ready:
        mixed(*u, prob)

    @pl.when((s > 0) & (old < (layers - 1) * nb))
    def _():
        out = mm(act_o[0], w2[...]).astype(BF).astype(F32)
        xbuf[rows_old, :] = (hid_o[0].astype(F32) + out).astype(BF)


def forward(x, wq, wk, wv, wo, w1, w2, tb=512):
    layers, d, _ = wq.shape
    ff = w1.shape[1]
    t = x.shape[0]
    nb = t // tb
    n = layers * nb
    prow = (tb // SEQ) * (d // PAIR) * SEQ
    once = pl.Buffered(1)

    def cur(s):
        return jnp.minimum(s, n - 1)

    def old(s):
        return jnp.maximum(s - 1, 0)

    def weight(at):
        return pl.BlockSpec((1, d, d), lambda s: (at(s) // nb, 0, 0))

    def tok(w, at, r=tb):
        return pl.BlockSpec((1, r, w), lambda s: (at(s) // nb, at(s) % nb, 0))

    def sds(w):
        return jax.ShapeDtypeStruct((layers, t, w), BF)

    return pl.pallas_call(
        functools.partial(fwd_body, layers=layers, nb=nb, tb=tb),
        grid=(n + 1,),
        in_specs=[pl.BlockSpec((tb, d), lambda s: (jnp.minimum(s, nb - 1), 0)), weight(cur), weight(cur), weight(cur), weight(old),
                  pl.BlockSpec((d, ff), lambda s: (0, 0), pipeline_mode=once),
                  pl.BlockSpec((ff, d), lambda s: (0, 0), pipeline_mode=once)],
        out_specs=[tok(d, cur), tok(d, cur), tok(d, cur), tok(d, cur), tok(2 * SEQ, cur, prow),
                   tok(d, cur), tok(d, old), tok(d, old), tok(ff, old), tok(ff, old)],
        out_shape=[sds(d), sds(d), sds(d), sds(d), jax.ShapeDtypeStruct((layers, nb * prow, 2 * SEQ), BF),
                   sds(d), sds(d), sds(d), sds(ff), sds(ff)],
        scratch_shapes=[pltpu.VMEM((t, d), BF), pltpu.VMEM((tb, d), BF)],
        compiler_params=pltpu.CompilerParams(dimension_semantics=("arbitrary",), vmem_limit_bytes=63 * 1024 * 1024),
        name="fwd_stack",
    )(x, wq, wk, wv, wo, w1, w2)


def rms_pull(v, dy):
    r = inv_rms(v)
    return dy * r - v * (r * r * r * jnp.mean(v * dy, axis=-1, keepdims=True))


def gelu_pull(x, d):
    sq = x * x
    t = jnp.tanh(x * (GC + (GC * GA) * sq))
    return d * (0.5 + 0.5 * t + (0.5 * x) * (1.0 - t * t) * (GC + (3.0 * GC * GA) * sq))


def bwd_body(dn_ref, hid_ref, pre_ref, x_ref, q_ref, k_ref, v_ref, p_ref, mix_ref, wq, wk, wv, wo, w1, w2,
             dx_o, keep_o, dpre_o, g_o, dhbuf, dmix, dq, dk, dv):
    @pl.when(pl.program_id(0) == 0)
    def _():
        g_o[...] = jnp.zeros_like(g_o)
        dhbuf[...] = jnp.zeros_like(dhbuf)
        dmix[...] = jnp.zeros_like(dmix)

    tb, d = dx_o.shape
    pairs = d // PAIR
    dn = dn_ref[...]
    keep_o[0] = dn
    hid = hid_ref[0].astype(F32)
    ff = w1.shape[1]
    step = BWD_CHUNK
    chunks = ff // step
    units = [(i, p) for i in range(tb // SEQ) for p in range(pairs)]
    each = -(-len(units) // chunks)

    def place(i, p):
        return slice(i * SEQ, (i + 1) * SEQ), slice(p * PAIR, (p + 1) * PAIR), (i * pairs + p) * SEQ

    def first(i, p):
        sl, lanes, at = place(i, p)
        d_mixed = stack_heads(dmix[sl, lanes])
        d_prob = mm(v_ref[0, sl, lanes], d_mixed, 1, 1)
        dv[sl, lanes] = mm(p_ref[0, at:at + SEQ, :], d_mixed, 1, 0).astype(BF)
        return d_prob

    def soft(i, p, d_prob):
        at = place(i, p)[2]
        d_prob = d_prob.astype(BF).astype(F32)
        prob = p_ref[0, at:at + SEQ, :].astype(F32)
        row = jnp.sum(d_prob * prob, axis=0, keepdims=True)
        return (prob * (d_prob - row) * SCALE).astype(BF)

    def second(i, p, d_st):
        sl, lanes, _ = place(i, p)
        dk[sl, lanes] = mm(d_st, stack_heads(q_ref[0, sl, lanes]), 1, 0).astype(BF)
        dq[sl, lanes] = mm(rows_of(d_st), stack_heads(k_ref[0, sl, lanes]), 0, 0).astype(BF)

    ready = []
    for j in range(chunks):
        group = units[j * each:(j + 1) * each]
        scores = [first(*u) for u in group]
        for u, d_st in ready:
            second(*u, d_st)
        cols = slice(j * step, (j + 1) * step)
        d_act = mm(dn, w2[cols, :], 1, 1)
        ready = [(u, soft(*u, d_prob)) for u, d_prob in zip(group, scores)]
        dpre_o[0, :, cols] = gelu_pull(pre_ref[0, :, cols].astype(F32), d_act.astype(BF).astype(F32)).astype(BF)
    for u, d_st in ready:
        second(*u, d_st)
    dh = dhbuf[...]
    g_o[3] += mm(mix_ref[0], dh, 0, 0)
    d_n2 = mm(dpre_o[0], w1[...], 1, 1).astype(BF).astype(F32)
    x = x_ref[0].astype(F32)
    normed = (x * inv_rms(x)).astype(BF)
    g_o[0] += mm(normed, dq[...], 0, 0)
    g_o[1] += mm(normed, dk[...], 0, 0)
    g_o[2] += mm(normed, dv[...], 0, 0)
    dh_new = (dn.astype(F32) + rms_pull(hid, d_n2)).astype(BF)
    d_n1 = (mm(dq[...], wq[0], 1, 1) + mm(dk[...], wk[0], 1, 1) + mm(dv[...], wv[0], 1, 1)).astype(BF).astype(F32)
    dx_o[...] = (dh.astype(F32) + rms_pull(x, d_n1)).astype(BF)
    dmix[...] = mm(dh_new, wo[0], 1, 1).astype(BF)
    dhbuf[...] = dh_new


def backward(layer, d_next, xs, q, k, v, p, mix, hid, pre, wq, wk, wv, wo, w1, w2, tb=256):
    layers, d, _ = wq.shape
    ff = w1.shape[1]
    t = d_next.shape[0]
    nb = t // tb
    prow = (tb // SEQ) * (d // PAIR) * SEQ
    once = pl.Buffered(1)
    wspec = pl.BlockSpec((1, d, d), lambda b: (layer, 0, 0), pipeline_mode=once)

    def cur(b):
        return jnp.minimum(b, nb - 1)

    def old(b):
        return jnp.maximum(b - 1, 0)

    def tok(w, at, r=tb):
        return pl.BlockSpec((1, r, w), lambda b: (layer, at(b), 0))

    def flat(at):
        return pl.BlockSpec((tb, d), lambda b: (at(b), 0))

    return pl.pallas_call(
        bwd_body,
        grid=(nb + 1,),
        in_specs=[flat(cur), tok(d, cur), tok(ff, cur), tok(d, old), tok(d, old), tok(d, old), tok(d, old), tok(2 * SEQ, old, prow),
                  tok(d, old), wspec, wspec, wspec, wspec,
                  pl.BlockSpec((d, ff), lambda b: (0, 0), pipeline_mode=once),
                  pl.BlockSpec((ff, d), lambda b: (0, 0), pipeline_mode=once)],
        out_specs=[flat(old), tok(d, cur), tok(ff, cur), pl.BlockSpec((4, d, d), lambda b: (0, 0, 0), pipeline_mode=once)],
        out_shape=[jax.ShapeDtypeStruct((t, d), BF), jax.ShapeDtypeStruct(hid.shape, BF), jax.ShapeDtypeStruct(pre.shape, BF),
                   jax.ShapeDtypeStruct((4, d, d), F32)],
        input_output_aliases={1: 1, 2: 2},
        scratch_shapes=[pltpu.VMEM((tb, d), BF)] * 5,
        cost_estimate=pl.CostEstimate(flops=80 * 10 ** 9, transcendentals=0, bytes_accessed=150 * 10 ** 6),
        compiler_params=pltpu.CompilerParams(dimension_semantics=("arbitrary",), vmem_limit_bytes=63 * 1024 * 1024),
        name="bwd_layer",
    )(d_next, hid, pre, xs, q, k, v, p, mix, wq, wk, wv, wo, w1, w2)


def local_step(x_init, cot_out, w_query, w_key, w_value, w_proj, w_up, w_down):
    layers, width, _ = w_query.shape
    x = x_init.reshape(-1, width)
    weights = (w_query, w_key, w_value, w_proj, w_up, w_down)
    xs, q, k, v, p, mix, hid, n2, pre, act = forward(x, *weights)
    d_act = cot_out.reshape(-1, width)
    sums = [None] * layers
    last = None
    for layer in reversed(range(layers)):
        d_act, hid, pre, part = backward(layer, d_act, xs, q, k, v, p, mix, hid, pre, *weights)
        if last is not None:
            part, last = lax.optimization_barrier((part, last))
            sums[layer + 1] = last
        last = lax.psum(part, "data")
    tall = lambda a: a.reshape(-1, a.shape[-1])
    g_up = mm(tall(n2), tall(pre), 0, 0)
    g_up, last = lax.optimization_barrier((g_up, last))
    sums[0] = last
    g_up = lax.psum(g_up, "data")
    g_down = mm(tall(act), tall(hid), 0, 0)
    g_down, g_up = lax.optimization_barrier((g_down, g_up))
    g_down = lax.psum(g_down, "data")
    attn = [jnp.stack([part[i] for part in sums]) for i in range(4)]
    return (*attn, g_up, g_down, d_act.reshape(x_init.shape))


def solution(mesh):
    data_spec = P("data")
    full_spec = P()
    in_specs = (data_spec, data_spec) + (full_spec,) * 6
    out_specs = (full_spec,) * 6 + (data_spec,)
    return jax.shard_map(local_step, mesh=mesh, in_specs=in_specs, out_specs=out_specs, check_vma=False)
```

time: 2120 us -> 1760 us (0.83)
  Pallas kernels: 1700 us -> 1340 us
    pallas_call x7, Pallas kernels: 1700 us -> 1340 us  [the longest x6 831 us: backward(): pl.pallas_call(bwd_body, grid=(nb + 1,), in_specs=[flat(cur), tok(d, cur)...]
  transfers between devices with their start and end apart: 8 -> 8, of which waited for: 1 -> 1; matrix products, arithmetic and copies ran while one was open for 14% -> 17% of each run, Pallas kernels for 42% -> 39%
where the time goes in v2:
time: 1760 us
  Pallas kernels  1340 us (76%)
  matrix products  263 us (15%)
  waiting for transfers between devices  90.1 us (5%)
  local copies, waits for them, and re-layouts  51.7 us (3%)
    pallas_call x6, Pallas kernels, backward(): pl.pallas_call(bwd_body, grid=(nb + 1,), in_specs=[flat(cur), tok(d, cur)...  831 us
    pallas_call x1, Pallas kernels, forward(): pl.pallas_call(functools.partial(fwd_body, layers=layers, nb=nb, tb=tb),...  508 us
    dot_general x2, matrix products, mm(): lax.dot_general(a, b, (((ca,), (cb,)), ((), ())), preferred_element_type=...  263 us
    psum x1, waiting for transfers between devices, local_step(): g_down = lax.psum(g_down, 'data')  89.9 us
    unnamed x37, local copies, waits for them, and re-layouts  47.9 us
  transfers between devices with their start and end apart: 8, of which 1 were waited for; matrix products, arithmetic and copies ran while one was open for 17% of the time, Pallas kernels for 39%

profile of v2, /device:TPU:0, one launch (start us, length us, event | category | flops | bytes accessed | tf_op | source)
XLA Modules:
  0.0 1758.2 jit_solution(409303292282889521)
XLA Ops:
  7.2 0.0 all-reduce.9.cloned.1.call-start
  7.2 507.7 %fwd_stack.1 = (bf16[6,4096,768]{2,1,0:T(8,128)(2,1)}, bf16[6,4096,768]{2,1,0:T(8,128)(2,1)}, bf16[6,4096,768]{2,1,0:T(8,128)(2,1)}, bf16[6,4096,768]{2,1,0:T(8,...) custom-call(bf16[4096,768]{1,0:T(8,128)(2,1)} %bitcast.22, ...), custom_call_target="tpu_custom_call" | custom-call | tf_op jit(solution)/shard_map/fwd_stack/pallas_call | solution.py:146
  514.9 138.5 %bwd_layer.6 = (bf16[4096,768]{1,0:T(8,128)(2,1)}, bf16[6,4096,768]{2,1,0:T(8,128)(2,1)}, bf16[6,4096,3072]{2,1,0:T(8,128)(2,1)}, f32[4,768,768]{2,1,0:T(8,128)}) custom-call(bf16[4096,768]{1,0:T(8,128)(2,1)} %bitcast.21, bf16[6,4096,768]{2,1,0:T(8,128)(2,1)} %get-tuple-element.56.hid_ref, ...), custom_call_target="tpu_custom_call", output_to_operand_aliasing={{1}: (1, {}), {2}: (2, {})} | custom-call | flops 80000000000 | bytes 150000000 | tf_op jit(solution)/shard_map/bwd_layer/pallas_call | solution.py:262
  653.4 0.0 all-reduce.9.cloned.1.call-update
  653.5 0.0 all-reduce.11.cloned.1.call-start
  653.5 138.2 %bwd_layer.7 = (bf16[4096,768]{1,0:T(8,128)(2,1)}, bf16[6,4096,768]{2,1,0:T(8,128)(2,1)}, bf16[6,4096,3072]{2,1,0:T(8,128)(2,1)}, f32[4,768,768]{2,1,0:T(8,128)}) custom-call(bf16[4096,768]{1,0:T(8,128)(2,1)} %get-tuple-element.64.dn_ref, bf16[6,4096,768]{2,1,0:T(8,128)(2,1)} %get-tuple-element.65.hid_ref, ...), custom_call_target="tpu_custom_call", output_to_operand_aliasing={{1}: (1, {}), {2}: (2, {})} | custom-call | flops 80000000000 | bytes 150000000 | tf_op jit(solution)/shard_map/bwd_layer/pallas_call | solution.py:262
  791.7 0.0 all-reduce.9.cloned.1.call-done
  791.7 0.0 all-reduce.11.cloned.1.call-update
  791.7 0.0 all-reduce.13.cloned.1.call-start
  791.8 138.5 %bwd_layer.8 = (bf16[4096,768]{1,0:T(8,128)(2,1)}, bf16[6,4096,768]{2,1,0:T(8,128)(2,1)}, bf16[6,4096,3072]{2,1,0:T(8,128)(2,1)}, f32[4,768,768]{2,1,0:T(8,128)}) custom-call(bf16[4096,768]{1,0:T(8,128)(2,1)} %get-tuple-element.67.dn_ref, bf16[6,4096,768]{2,1,0:T(8,128)(2,1)} %get-tuple-element.68.hid_ref, ...), custom_call_target="tpu_custom_call", output_to_operand_aliasing={{1}: (1, {}), {2}: (2, {})} | custom-call | flops 80000000000 | bytes 150000000 | tf_op jit(solution)/shard_map/bwd_layer/pallas_call | solution.py:262
  930.3 0.0 all-reduce.11.cloned.1.call-done
  930.3 0.0 all-reduce.13.cloned.1.call-update
  930.3 0.0 all-reduce.15.cloned.1.call-start
  930.4 138.4 %bwd_layer.9 = (bf16[4096,768]{1,0:T(8,128)(2,1)}, bf16[6,4096,768]{2,1,0:T(8,128)(2,1)}, bf16[6,4096,3072]{2,1,0:T(8,128)(2,1)}, f32[4,768,768]{2,1,0:T(8,128)}) custom-call(bf16[4096,768]{1,0:T(8,128)(2,1)} %get-tuple-element.70.dn_ref, bf16[6,4096,768]{2,1,0:T(8,128)(2,1)} %get-tuple-element.71.hid_ref, ...), custom_call_target="tpu_custom_call", output_to_operand_aliasing={{1}: (1, {}), {2}: (2, {})} | custom-call | flops 80000000000 | bytes 150000000 | tf_op jit(solution)/shard_map/bwd_layer/pallas_call | solution.py:262
  1068.8 0.0 all-reduce.13.cloned.1.call-done
  1068.8 0.0 all-reduce.15.cloned.1.call-update
  1068.9 0.0 all-reduce.17.cloned.1.call-start
  1068.9 138.5 %bwd_layer.10 = (bf16[4096,768]{1,0:T(8,128)(2,1)}, bf16[6,4096,768]{2,1,0:T(8,128)(2,1)}, bf16[6,4096,3072]{2,1,0:T(8,128)(2,1)}, f32[4,768,768]{2,1,0:T(8,128)}) custom-call(bf16[4096,768]{1,0:T(8,128)(2,1)} %get-tuple-element.73.dn_ref, bf16[6,4096,768]{2,1,0:T(8,128)(2,1)} %get-tuple-element.74.hid_ref, ...), custom_call_target="tpu_custom_call", output_to_operand_aliasing={{1}: (1, {}), {2}: (2, {})} | custom-call | flops 80000000000 | bytes 150000000 | tf_op jit(solution)/shard_map/bwd_layer/pallas_call | solution.py:262
  1207.4 0.0 all-reduce.15.cloned.1.call-done
  1207.5 0.0 all-reduce.17.cloned.1.call-update
  1207.5 0.0 all-reduce.19.cloned.1.call-start
  1207.5 138.4 %bwd_layer.11 = (bf16[4096,768]{1,0:T(8,128)(2,1)}, bf16[6,4096,768]{2,1,0:T(8,128)(2,1)}, bf16[6,4096,3072]{2,1,0:T(8,128)(2,1)}, f32[4,768,768]{2,1,0:T(8,128)}) custom-call(bf16[4096,768]{1,0:T(8,128)(2,1)} %get-tuple-element.76.dn_ref, bf16[6,4096,768]{2,1,0:T(8,128)(2,1)} %get-tuple-element.77.hid_ref, ...), custom_call_target="tpu_custom_call", output_to_operand_aliasing={{1}: (1, {}), {2}: (2, {})} | custom-call | flops 80000000000 | bytes 150000000 | tf_op jit(solution)/shard_map/bwd_layer/pallas_call | solution.py:262
  1345.9 0.0 all-reduce.17.cloned.1.call-done
  1345.9 0.0 all-reduce.19.cloned.1.call-update
  1346.0 0.0 all-reduce.21.cloned.1.call-start
  1346.0 129.6 %convolution_bitcast_fusion.1 = f32[768,3072]{1,0:T(8,128)} fusion(bf16[6,4096,768]{2,1,0:T(8,128)(2,1)} %get-tuple-element.55, bf16[6,4096,3072]{2,1,0:T(8,128)(2,1)} %get-tuple-element.79), kind=kOutput, calls=%fused_computation.1 | convolution fusion | flops 115964116992 | bytes 198180864 | tf_op jit(solution)/shard_map/dot_general | solution.py:25
  1475.6 0.0 all-reduce.19.cloned.1.call-done
  1475.6 0.0 all-reduce.21.cloned.1.call-update
  1475.6 0.0 all-reduce.23.cloned.1.call-start
  1475.7 133.6 %convolution_bitcast_fusion = f32[3072,768]{1,0:T(8,128)} fusion(bf16[6,4096,3072]{2,1,0:T(8,128)(2,1)} %get-tuple-element.97, bf16[6,4096,768]{2,1,0:T(8,128)(2,1)} %get-tuple-element.98), kind=kOutput, calls=%fused_computation | convolution fusion | flops 115964116992 | bytes 198180864 | tf_op jit(solution)/shard_map/dot_general | solution.py:25
  1609.2 0.0 all-reduce.21.cloned.1.call-done
  1609.3 0.0 all-reduce.23.cloned.1.call-update
  1609.3 7.6 slice_dynamic-update-slice_fusion.5
  1616.9 0.0 slice-start.9
  1616.9 0.0 slice-start.10
  1616.9 0.0 slice-start.11
  1616.9 8.7 slice_dynamic-update-slice_fusion.4
  1625.6 0.0 slice-start.6
  1625.6 0.0 slice-done.9
  1625.6 0.3 slice-done.10
  1625.8 0.7 slice-done.11
  1626.6 0.0 slice-start.7
  1626.6 0.0 slice-start.8
  1626.6 4.8 slice_dynamic-update-slice_fusion.3
  1631.4 0.0 slice-start.3
  1631.4 0.0 slice-done.6
  1631.4 0.9 slice-done.7
  1632.3 0.4 slice-done.8
  1632.7 0.0 slice-start.4
  1632.7 4.8 slice_dynamic-update-slice_fusion.2
  1637.5 0.0 slice-done.3
  1637.5 0.4 slice-done.4
  1637.9 0.8 slice-done.5
  1638.7 4.8 slice_dynamic-update-slice_fusion.1
  1643.5 0.0 slice-done
  1643.5 0.3 slice-done.1
  1643.8 0.9 slice-done.2
  1644.7 3.8 slice_dynamic-update-slice_fusion
  1648.5 89.9 %all-reduce.23.cloned.1.call-done = f32[3072,768]{1,0:T(8,128)} async-done(((f32[3072,768]{1,0:T(8,128)}), f32[3072,768]{1,0:T(8,128)}) %all-reduce.23.cloned.1.call-update) | async-done | bytes 9437200 | tf_op jit(solution)/shard_map/psum | solution.py:301
  1738.4 8.8 copy.71
  1747.1 0.0 slice-done.12
  1747.1 0.0 slice-done.13
  1747.1 0.0 slice-done.14
  1747.1 3.7 copy.72
  (12 shorter events, 0.0 us)
Async XLA Ops:
  7.2 784.5 %all-reduce.9.cloned.1.call-start = ((), (), s32[]{:S(2)}) async-start(), calls=%async_computation | async-start | bytes 18874368 | tf_op jit(solution)/shard_map/psum | solution.py:293
  653.5 276.9 %all-reduce.11.cloned.1.call-start = ((), (), s32[]{:S(2)}) async-start(), calls=%async_computation.1 | async-start | bytes 18874368 | tf_op jit(solution)/shard_map/psum | solution.py:293
  791.7 277.1 %all-reduce.13.cloned.1.call-start = ((), (), s32[]{:S(2)}) async-start(), calls=%async_computation.2 | async-start | bytes 18874368 | tf_op jit(solution)/shard_map/psum | solution.py:293
  930.3 277.1 %all-reduce.15.cloned.1.call-start = ((), (), s32[]{:S(2)}) async-start(), calls=%async_computation.3 | async-start | bytes 18874368 | tf_op jit(solution)/shard_map/psum | solution.py:293
  1068.9 277.0 %all-reduce.17.cloned.1.call-start = ((), (), s32[]{:S(2)}) async-start(), calls=%async_computation.4 | async-start | bytes 18874368 | tf_op jit(solution)/shard_map/psum | solution.py:293
  1207.5 268.1 %all-reduce.19.cloned.1.call-start = ((), (), s32[]{:S(2)}) async-start(), calls=%async_computation.5 | async-start | bytes 18874368 | tf_op jit(solution)/shard_map/psum | solution.py:293
  1346.0 263.3 %all-reduce.21.cloned.1.call-start = ((), (), s32[]{:S(2)}) async-start(), calls=%async_computation.6 | async-start | bytes 18874368 | tf_op jit(solution)/shard_map/psum | solution.py:298
  1475.6 262.7 %all-reduce.23.cloned.1.call-start = ((), (), s32[]{:S(2)}) async-start(), calls=%async_computation.7 | async-start | bytes 18874368 | tf_op jit(solution)/shard_map/psum | solution.py:301
  1616.9 8.7 slice-start.9
  1616.9 9.0 slice-start.10
  1616.9 9.7 slice-start.11
  1625.6 5.8 slice-start.6
  1626.6 5.7 slice-start.7
  1626.6 6.1 slice-start.8
  1631.4 6.1 slice-start.3
  1632.7 5.2 slice-start.4
  1632.7 6.0 slice-start.5
  1637.5 6.0 slice-start
  1638.7 5.1 slice-start.1
  1638.7 6.0 slice-start.2
  1738.4 8.8 slice-start.12
  1738.4 8.8 slice-start.13
  1738.4 8.8 slice-start.14
Sparse Core Ops, SparseCore 0:
  653.6 128.9 all-reduce.8
  791.9 128.9 all-reduce.10
  930.5 128.9 all-reduce.12
  1069.0 128.9 all-reduce.14
  1207.6 128.9 all-reduce.16
  1346.1 128.9 all-reduce.18
  1479.1 126.1 all-reduce.20
  1609.4 128.9 all-reduce.22
